TPU v7x, 32 devices: a whole 2x2x4 slice. The times are simulated.
32 devices in a mesh: gx: 4 (over y, x), gy: 8 (over z, core).
Axes of the slice: x: 2, y: 2, z: 4, core: 2. Of those that a mesh axis runs over, the one named last changes fastest.
Arguments:
- species_means: bfloat16 [8, 16, 120, 512], P(None, 'gy', None, 'gx'), may hold values from 0.19921875 to 5
- zonal_edge_velocity: float32 [16, 120, 512], P('gy', None, 'gx'), may hold values from -6 to 6
- meridional_edge_velocity: float32 [16, 120, 512], P('gy', None, 'gx'), may hold values from -6 to 6
- scaled_warmth: float32 [16, 120, 512], P('gy', None, 'gx'), may hold values from 0.5 to 2
- donor_depths: float32 [16, 120, 512], P('gy', None, 'gx'), may hold values from 0.5 to 2
- leading_donor_level: int32 [16, 120, 512], P('gy', None, 'gx'), may hold values from 0 to 118, as said below
- opening_share: bfloat16 [16, 120, 512], P('gy', None, 'gx'), may hold values from 0 to 0.44921875
- closing_share: bfloat16 [16, 120, 512], P('gy', None, 'gx'), may hold values from 0.546875 to 1
Outputs:
- tracers_out: float32 [8, 16, 120, 512], P(None, 'gy', None, 'gx')
- regridded_zonal: float32 [16, 120, 512], P('gy', None, 'gx')
- regridded_meridional: float32 [16, 120, 512], P('gy', None, 'gx')
- adjusted_warmth: float32 [16, 120, 512], P('gy', None, 'gx')
Inputs may be any that keep to these rules, and one draw needn't show every extreme that they name: Target layer k draws on source layers leading_donor_level and leading_donor_level + 1, and leading_donor_level lies within 2 of k.
All inputs are finite; a program needn't handle non-finite values.
Results may differ from a plain program's by a relative error of at most 0.0003.
Values sent between devices are 32-bit elements; how exact they have to be, the bound alone decides.
A program may use at most 64 MiB of HBM per device.

v0:
```python
import jax
import jax.numpy as jnp
from jax import lax
from jax.sharding import PartitionSpec as P

thermal_rescale_factor = 3.5
offsets_all = (-2, -1, 0, 1, 2, 3)


def passed_along(value, axis, steps):
    count = lax.axis_size(axis)
    pairs = [(source, (source + steps) % count) for source in range(count)]
    return lax.ppermute(value, axis, pairs)


def ppm_parts(values):
    layers = values.shape[-2]
    top_edge = 1.5 * values[..., 0:1, :] - 0.5 * values[..., 1:2, :]
    second_edge = 0.5 * (values[..., 0:1, :] + values[..., 1:2, :])
    inner_edge = 7.0 / 12.0 * (
        values[..., 1 : layers - 2, :] + values[..., 2 : layers - 1, :]
    ) - 1.0 / 12.0 * (values[..., 0 : layers - 3, :] + values[..., 3:layers, :])
    lower_edge = 0.5 * (
        values[..., layers - 2 : layers - 1, :] + values[..., layers - 1 : layers, :]
    )
    bottom_edge = (
        1.5 * values[..., layers - 1 : layers, :] - 0.5 * values[..., layers - 2 : layers - 1, :]
    )
    edge_values = jnp.concatenate(
        [top_edge, second_edge, inner_edge, lower_edge, bottom_edge], axis=-2
    )
    left_edge = edge_values[..., :layers, :]
    right_edge = edge_values[..., 1:, :]
    return (left_edge, right_edge - left_edge, 6.0 * values - 3.0 * (left_edge + right_edge))


def shifted_layers(values, amount):
    layers = values.shape[-2]
    if amount == 0:
        return values
    if amount > 0:
        filler = jnp.zeros(values.shape[:-2] + (amount, values.shape[-1]), values.dtype)
        return jnp.concatenate([values[..., amount:, :], filler], axis=-2)
    filler = jnp.zeros(values.shape[:-2] + (-amount, values.shape[-1]), values.dtype)
    return jnp.concatenate([filler, values[..., : layers + amount, :]], axis=-2)


def pick_layers(values, masks):
    total = jnp.zeros(values.shape, jnp.float32)
    for amount, selector in zip(offsets_all, masks):
        total = total + jnp.where(selector, shifted_layers(values, amount), 0.0)
    return total


def build_operator(donor_depths, leading_donor_level, opening_share, closing_share):
    start_frac = opening_share.astype(jnp.float32)
    end_frac = closing_share.astype(jnp.float32)
    layer_offset = leading_donor_level - lax.broadcasted_iota(
        jnp.int32, leading_donor_level.shape, 1
    )
    first_masks = [layer_offset == amount for amount in offsets_all]
    second_masks = [layer_offset + 1 == amount for amount in offsets_all]
    weight_first = (1.0 - start_frac) * pick_layers(donor_depths, first_masks)
    weight_second = end_frac * pick_layers(donor_depths, second_masks)
    linear_first = 0.5 * (start_frac + 1.0)
    square_first = linear_first - (start_frac * start_frac + start_frac + 1.0) / 3.0
    linear_second = 0.5 * end_frac
    square_second = linear_second - end_frac * end_frac / 3.0
    return (
        first_masks,
        second_masks,
        weight_first,
        weight_second,
        linear_first,
        square_first,
        linear_second,
        square_second,
    )


def multiply_by_regrid_operator(operator, values):
    (
        first_masks,
        second_masks,
        weight_first,
        weight_second,
        linear_first,
        square_first,
        linear_second,
        square_second,
    ) = operator
    left_edge, edge_slope, curvature = ppm_parts(values)
    mean_first = (
        pick_layers(left_edge, first_masks)
        + pick_layers(edge_slope, first_masks) * linear_first
        + pick_layers(curvature, first_masks) * square_first
    )
    mean_second = (
        pick_layers(left_edge, second_masks)
        + pick_layers(edge_slope, second_masks) * linear_second
        + pick_layers(curvature, second_masks) * square_second
    )
    return (weight_first * mean_first + weight_second * mean_second) / (
        weight_first + weight_second
    )


def local(
    species_means,
    zonal_edge_velocity,
    meridional_edge_velocity,
    scaled_warmth,
    donor_depths,
    leading_donor_level,
    opening_share,
    closing_share,
):
    vertical_regrid_operator = build_operator(
        donor_depths, leading_donor_level, opening_share, closing_share
    )
    regridded_depths = vertical_regrid_operator[2] + vertical_regrid_operator[3]
    mass_before = jnp.sum(species_means.astype(jnp.float32) * donor_depths, axis=(1, 2, 3))
    interior_u_faces = 0.5 * jnp.sum(
        0.5
        * (donor_depths[:-1] + donor_depths[1:])
        * zonal_edge_velocity[:-1]
        * zonal_edge_velocity[:-1]
    )
    interior_v_faces = 0.5 * jnp.sum(
        0.5
        * (donor_depths[:, :, :-1] + donor_depths[:, :, 1:])
        * meridional_edge_velocity[:, :, :-1]
        * meridional_edge_velocity[:, :, :-1]
    )
    local_prior_totals = (
        thermal_rescale_factor * jnp.sum(donor_depths * scaled_warmth)
        + interior_u_faces
        + interior_v_faces
    )
    from_south = passed_along(zonal_edge_velocity[-1:], "gy", 1)
    u_paired = multiply_by_regrid_operator(
        vertical_regrid_operator,
        jnp.stack(
            [zonal_edge_velocity, jnp.concatenate([from_south, zonal_edge_velocity[:-1]], axis=0)]
        ),
    )
    u_cross = u_paired[1]
    returned = passed_along(
        jnp.stack([u_cross[0:1], donor_depths[0:1], regridded_depths[0:1]]), "gy", -1
    )
    north_thick = returned[2]
    edge_u = 0.5 * jnp.sum(
        0.5
        * (donor_depths[-1:] + returned[1])
        * zonal_edge_velocity[-1:]
        * zonal_edge_velocity[-1:]
    )
    regridded_zonal = 0.5 * (u_paired[0] + jnp.concatenate([u_cross[1:], returned[0]], axis=0))
    zonal_following = 0.5 * jnp.sum(
        0.5
        * (regridded_depths + jnp.concatenate([regridded_depths[1:], north_thick], axis=0))
        * regridded_zonal
        * regridded_zonal
    )
    from_west = passed_along(meridional_edge_velocity[:, :, -1:], "gx", 1)
    v_paired = multiply_by_regrid_operator(
        vertical_regrid_operator,
        jnp.stack(
            [
                meridional_edge_velocity,
                jnp.concatenate([from_west, meridional_edge_velocity[:, :, :-1]], axis=2),
            ]
        ),
    )
    v_cross = v_paired[1]
    v_returned = passed_along(
        jnp.stack([v_cross[:, :, 0:1], donor_depths[:, :, 0:1], regridded_depths[:, :, 0:1]]),
        "gx",
        -1,
    )
    regridded_meridional = 0.5 * (
        v_paired[0] + jnp.concatenate([v_cross[:, :, 1:], v_returned[0]], axis=2)
    )
    edge_v = 0.5 * jnp.sum(
        0.5
        * (donor_depths[:, :, -1:] + v_returned[1])
        * meridional_edge_velocity[:, :, -1:]
        * meridional_edge_velocity[:, :, -1:]
    )
    meridional_following = 0.5 * jnp.sum(
        0.5
        * (regridded_depths + jnp.concatenate([regridded_depths[:, :, 1:], v_returned[2]], axis=2))
        * regridded_meridional
        * regridded_meridional
    )
    tracer_new = multiply_by_regrid_operator(
        vertical_regrid_operator, species_means.astype(jnp.float32)
    )
    regridded_warmth = multiply_by_regrid_operator(vertical_regrid_operator, scaled_warmth)
    mass_after = jnp.sum(tracer_new * regridded_depths, axis=(1, 2, 3))
    aggregate_regridded = jnp.sum(regridded_depths)
    kinetic_thermal_following = (
        thermal_rescale_factor * jnp.sum(regridded_depths * regridded_warmth)
        + zonal_following
        + meridional_following
    )
    mass_total_before, mass_total_after, scalars = lax.psum(
        (
            mass_before,
            mass_after,
            jnp.stack(
                [
                    local_prior_totals + edge_u + edge_v,
                    kinetic_thermal_following,
                    aggregate_regridded,
                ]
            ),
        ),
        ("gx", "gy"),
    )
    enthalpy_global_preceding = scalars[0]
    enthalpy_global_following = scalars[1]
    thick_total = scalars[2]
    tracers_out = (
        tracer_new + ((mass_total_before - mass_total_after) / thick_total)[:, None, None, None]
    )
    adjusted_warmth = regridded_warmth + (enthalpy_global_preceding - enthalpy_global_following) / (
        thermal_rescale_factor * thick_total
    )
    return (tracers_out, regridded_zonal, regridded_meridional, adjusted_warmth)


def solution(mesh):
    in_specs = (
        P(None, "gy", None, "gx"),
        P("gy", None, "gx"),
        P("gy", None, "gx"),
        P("gy", None, "gx"),
        P("gy", None, "gx"),
        P("gy", None, "gx"),
        P("gy", None, "gx"),
        P("gy", None, "gx"),
    )
    out_specs = (
        P(None, "gy", None, "gx"),
        P("gy", None, "gx"),
        P("gy", None, "gx"),
        P("gy", None, "gx"),
    )
    return jax.shard_map(local, mesh=mesh, in_specs=in_specs, out_specs=out_specs, check_vma=False)
```

profile of v0, /device:TPU:0, one launch (start us, length us, event | category | flops | bytes accessed | tf_op | source)
XLA Modules:
  0.0 95.7 jit_solution(4133730569461327342)
XLA Ops:
  0.6 1.7 %slice.551 = f32[2,120,1]{2,1,0:T(8,128)} slice(f32[2,120,128]{2,1,0:T(8,128)} %param.10), slice={[0:2], [0:120], [127:128]} | slice | bytes 1920 | tf_op jit(solution)/shard_map/slice | solution.py:165
  2.3 3.0 %collective-permute-start.2 = (f32[2,120,1]{2,1,0:T(8,128)}, f32[2,120,1]{2,1,0:T(8,128)S(1)}, u32[]{:S(2)}, u32[]{:S(2)}) collective-permute-start(f32[2,120,1]{2,1,0:T(8,128)} %slice.551), channel_id=1, source_target_pairs={{0,8},{8,16},{16,24},{24,0},{1,9},{9,17},{17,25},{25,1},{2,10},{10... | collective-permute-start | bytes 2888 | tf_op jit(solution)/shard_map/ppermute | solution.py:13
  5.3 0.6 fusion.103
  6.0 1.0 %copy-done.2 = bf16[8,2,120,128]{3,2,1,0:T(8,128)(2,1)S(1)} copy-done((bf16[8,2,120,128]{3,2,1,0:T(8,128)(2,1)S(1)}, bf16[8,2,120,128]{3,2,1,0:T(8,128)(2,1)}, u32[]{:S(2)}) %copy-start.2) | copy-done | bytes 491544
  7.0 0.1 convert_element_type.11
  7.1 0.4 fusion.5
  7.5 0.6 fusion.7
  8.0 0.1 slice.631
  8.1 0.4 fusion.86
  8.5 0.4 fusion.87
  8.9 0.1 slice.626
  8.9 0.1 fusion
  9.0 0.1 pad_maximum_fusion.2
  9.1 0.0 copy-start.1
  9.1 0.1 pad_maximum_fusion.3
  9.2 0.8 copy-done.1
  10.0 0.8 fusion.46
  10.8 0.1 copy-done.12
  10.8 0.0 copy-done.13
  10.9 0.1 copy-done.15
  11.0 0.4 fusion.51
  11.4 0.1 slice_reduce_fusion
  11.5 0.0 copy-start.3
  11.5 0.7 fusion.102
  12.2 0.3 copy-done.3
  12.6 0.7 fusion.61
  13.3 0.8 fusion.98
  14.1 0.8 fusion.99
  14.9 0.7 fusion.40
  15.5 0.7 pad_maximum_fusion.20
  16.2 7.7 %multiply_reduce_fusion = (f32[8]{0:T(128)S(1)}, f32[8,2,120,128]{3,2,1,0:T(8,128)S(1)}) fusion(f32[2,120,128]{2,1,0:T(8,128)S(1)} %get-tuple-element.125, f32[2,120,128]{2,1,0:T(8,128)S(1)} %get-tuple-element.141, f32[2,120,128]{2,1,0:T(8,128)S(1)} %get-tuple-element.140, pred[2,120,128]{2,1,0:T(8,128)(4,1)S(1)} %get-tuple-element.127, ...), kind=kLoop, calls=%fused_computation.18 | loop fusion | flops 24084472 | bytes 17244192 | tf_op jit(solution)/shard_map/reduce_sum | solution.py:200
  24.0 0.8 slice.715
  24.7 0.7 slice.709
  25.4 0.7 slice.704
  26.0 0.1 copy.189
  27.4 0.1 maximum_bitcast_fusion.1
  27.5 0.1 fusion.19
  27.6 0.1 fusion.38
  28.1 1.0 %add_divide_fusion.1 = f32[2,2,120,128]{3,2,1,0:T(8,128)S(1)} fusion(f32[2,2,120,128]{3,2,1,0:T(8,128)S(1)} %get-tuple-element.71, f32[2,2,117,128]{3,2,1,0:T(8,128)S(1)} %slice.692, f32[2,2,118,128]{3,2,1,0:T(8,128)S(1)} %get-tuple-element.90, f32[2,2,119,128]{3,2,1,0:T(8,128)S(1)} %get-tuple-element.92, f32[2,2,119,128]{3,2,1,0:T(8,128)S(1)} %get-tuple-element.91, ...), kind=kLoop, calls=%fused_computation.105 | loop fusion | flops 5591040 | bytes 5355520 | tf_op jit(solution)/shard_map/div | solution.py:103
  29.1 0.1 slice_reduce_fusion.1
  29.2 0.7 slice.718
  29.9 1.2 %collective-permute-start.3 = (f32[3,2,120,1]{2,1,3,0:T(2,128)S(1)}, f32[3,2,120,1]{2,1,3,0:T(2,128)S(1)}, u32[]{:S(2)}, u32[]{:S(2)}) collective-permute-start(f32[3,2,120,1]{2,1,3,0:T(2,128)S(1)} %pad_maximum_fusion.23), channel_id=1, source_target_pairs={{0,24},{8,0},{16,8},{24,16},{1,25},{9,1},{17,9},{25,17},{2,26},{10... | collective-permute-start | bytes 8648 | tf_op jit(solution)/shard_map/ppermute | solution.py:13
  31.1 0.8 maximum_bitcast_fusion
  32.0 0.1 fusion.30
  32.1 0.1 fusion.39
  32.6 1.0 %add_divide_fusion.2 = f32[2,2,120,128]{3,2,1,0:T(8,128)S(1)} fusion(f32[2,2,120,128]{3,2,1,0:T(8,128)S(1)} %get-tuple-element.69, f32[2,2,117,128]{3,2,1,0:T(8,128)S(1)} %slice.660, f32[2,2,118,128]{3,2,1,0:T(8,128)S(1)} %get-tuple-element.79, f32[2,2,119,128]{3,2,1,0:T(8,128)S(1)} %get-tuple-element.81, f32[2,2,119,128]{3,2,1,0:T(8,128)S(1)} %get-tuple-element.80, ...), kind=kLoop, calls=%fused_computation.106 | loop fusion | flops 5591040 | bytes 5355520 | tf_op jit(solution)/shard_map/div | solution.py:103
  33.6 0.6 slice_bitcast_fusion.4
  34.2 0.2 copy-done.11
  34.4 0.7 pad_maximum_fusion.17
  35.1 3.0 %collective-permute-start.1 = (f32[3,1,120,128]{3,2,1,0:T(8,128)}, f32[3,1,120,128]{3,2,1,0:T(8,128)}, u32[]{:S(2)}, u32[]{:S(2)}) collective-permute-start(f32[3,1,120,128]{3,2,1,0:T(8,128)} %pad_maximum_fusion.17), channel_id=1, source_target_pairs={{0,7},{1,0},{2,1},{3,2},{4,3},{5,4},{6,5},{7,6},{8,15},{9,8},{10,9... | collective-permute-start | bytes 552968 | tf_op jit(solution)/shard_map/ppermute | solution.py:13
  38.1 0.8 copy.187
  38.9 0.8 copy.188
  39.7 0.1 copy.180
  39.8 0.8 fusion.47
  41.3 0.1 collective-permute-done.1
  41.4 0.9 slice_bitcast_fusion.3
  42.4 3.6 %fusion.49 = (f32[]{:T(128)}, f32[]{:T(128)}, f32[]{:T(128)}, f32[]{:T(128)}, f32[2,120,128]{2,1,0:T(8,128)}, /*index=5*/f32[2,120,128]{2,1,0:T(8,128)}, f32[2,120,128]{2,1,0:T(8,128)}) fusion(f32[2,120,128]{2,1,0:T(8,128)S(1)} %get-tuple-element.125, f32[2,120,1]{2,1,0:T(8,128)} %copy.187, f32[2,120,127]{2,1,0:T(8,128)} %slice.715, ...), kind=kLoop, calls=%fused_computation.136 | loop fusion | flops 3839996 | bytes 3906576 | tf_op jit(solution)/shard_map/reduce_sum | solution.py:190
  47.9 1.5 %fusion.63 = (f32[]{:T(128)}, f32[]{:T(128)}) fusion(f32[3,1,120,128]{3,2,1,0:T(8,128)} %collective-permute-done.1, f32[2,120,128]{2,1,0:T(8,128)S(1)} %copy-done, f32[2,120,128]{2,1,0:T(8,128)S(1)} %copy-done.4), kind=kLoop, calls=%fused_computation.176 | loop fusion | flops 153598 | bytes 307208 | tf_op jit(solution)/shard_map/reduce_sum | solution.py:152
  50.7 0.6 pad_maximum_fusion.24
  51.3 39.4 %all-reduce.65 = (f32[8]{0:T(128)S(1)}, f32[8]{0:T(128)S(1)}, f32[3]{0:T(128)S(1)}) all-reduce(f32[8]{0:T(128)S(1)} %get-tuple-element.67, f32[8]{0:T(128)S(1)} %get-tuple-element.36, f32[3]{0:T(128)S(1)} %pad_maximum_fusion.24), channel_id=1, replica_groups=mesh['gx'=4,'gy'=8] {'gx','gy'}, use_global_device_ids=true, to_apply=%region_1.2 | all-reduce | flops 19 | bytes 152 | tf_op jit(solution)/shard_map/psum | solution.py:207
  90.7 0.6 fusion.106
  92.0 0.7 subtract_divide_fusion
  92.7 1.1 %broadcast_add_fusion = f32[8,2,120,128]{3,2,1,0:T(8,128)} fusion(f32[8,2,120,128]{3,2,1,0:T(8,128)S(1)} %get-tuple-element.37, f32[8]{0:T(128)S(1)} %subtract_divide_fusion), kind=kLoop, calls=%fused_computation.57 | loop fusion | flops 245760 | bytes 1966112 | tf_op jit(solution)/shard_map/add | solution.py:225
  95.1 0.7 broadcast_add_fusion.1
  (62 shorter events, 0.8 us)
Async XLA Ops:
  0.6 4.7 %copy-start.4 = (f32[2,120,128]{2,1,0:T(8,128)S(1)}, f32[2,120,128]{2,1,0:T(8,128)}, u32[]{:S(2)}) copy-start(f32[2,120,128]{2,1,0:T(8,128)} %param.9) | copy-start | bytes 368644
  2.3 3.6 %copy-start = (f32[2,120,128]{2,1,0:T(8,128)S(1)}, f32[2,120,128]{2,1,0:T(8,128)}, u32[]{:S(2)}) copy-start(f32[2,120,128]{2,1,0:T(8,128)} %param.12) | copy-start | bytes 368644
  2.3 25.1 %collective-permute-start.2 = (f32[2,120,1]{2,1,0:T(8,128)}, f32[2,120,1]{2,1,0:T(8,128)S(1)}, u32[]{:S(2)}, u32[]{:S(2)}) collective-permute-start(f32[2,120,1]{2,1,0:T(8,128)} %slice.551), channel_id=1, source_target_pairs={{0,8},{8,16},{16,24},{24,0},{1,9},{9,17},{17,25},{25,1},{2,10},{10... | collective-permute-start | bytes 2888 | tf_op jit(solution)/shard_map/ppermute | solution.py:13
  5.9 25.2 %collective-permute-start = (f32[1,120,128]{2,1,0:T(8,128)}, f32[1,120,128]{2,1,0:T(8,128)}, u32[]{:S(2)}, u32[]{:S(2)}) collective-permute-start(f32[1,120,128]{2,1,0:T(8,128)} %get-tuple-element.117), channel_id=1, source_target_pairs={{0,1},{1,2},{2,3},{3,4},{4,5},{5,6},{6,7},{7,0},{8,9},{9,10},{10,1... | collective-permute-start | bytes 184328 | tf_op jit(solution)/shard_map/ppermute | solution.py:13
  6.0 1.0 %copy-start.2 = (bf16[8,2,120,128]{3,2,1,0:T(8,128)(2,1)S(1)}, bf16[8,2,120,128]{3,2,1,0:T(8,128)(2,1)}, u32[]{:S(2)}) copy-start(bf16[8,2,120,128]{3,2,1,0:T(8,128)(2,1)} %param.8) | copy-start | bytes 1474564
  9.1 0.9 copy-start.1
  10.0 0.8 copy-start.12
  10.0 0.9 copy-start.13
  10.0 1.0 %copy-start.15 = (s32[2,120,128]{2,1,0:T(8,128)S(1)}, s32[2,120,128]{2,1,0:T(8,128)}, u32[]{:S(2)}) copy-start(s32[2,120,128]{2,1,0:T(8,128)} %param.13) | copy-start | bytes 368644
  11.5 1.0 copy-start.3
  29.9 8.1 %collective-permute-start.3 = (f32[3,2,120,1]{2,1,3,0:T(2,128)S(1)}, f32[3,2,120,1]{2,1,3,0:T(2,128)S(1)}, u32[]{:S(2)}, u32[]{:S(2)}) collective-permute-start(f32[3,2,120,1]{2,1,3,0:T(2,128)S(1)} %pad_maximum_fusion.23), channel_id=1, source_target_pairs={{0,24},{8,0},{16,8},{24,16},{1,25},{9,1},{17,9},{25,17},{2,26},{10... | collective-permute-start | bytes 8648 | tf_op jit(solution)/shard_map/ppermute | solution.py:13
  33.5 0.8 copy-start.11
  35.1 6.4 %collective-permute-start.1 = (f32[3,1,120,128]{3,2,1,0:T(8,128)}, f32[3,1,120,128]{3,2,1,0:T(8,128)}, u32[]{:S(2)}, u32[]{:S(2)}) collective-permute-start(f32[3,1,120,128]{3,2,1,0:T(8,128)} %pad_maximum_fusion.17), channel_id=1, source_target_pairs={{0,7},{1,0},{2,1},{3,2},{4,3},{5,4},{6,5},{7,6},{8,15},{9,8},{10,9... | collective-permute-start | bytes 552968 | tf_op jit(solution)/shard_map/ppermute | solution.py:13
  38.9 3.4 %copy-start.7 = (f32[2,118,128]{2,1,0:T(8,128)S(1)}, f32[2,118,128]{2,1,0:T(8,128)}, u32[]{:S(2)}) copy-start(f32[2,118,128]{2,1,0:T(8,128)} %get-tuple-element.156) | copy-start | bytes 362500
  38.9 3.5 %copy-start.8 = (f32[2,118,128]{2,1,0:T(8,128)S(1)}, f32[2,118,128]{2,1,0:T(8,128)}, u32[]{:S(2)}) copy-start(f32[2,118,128]{2,1,0:T(8,128)} %get-tuple-element.157) | copy-start | bytes 362500
  38.9 3.5 %copy-start.14 = (f32[1,120,128]{2,1,0:T(8,128)S(1)}, f32[1,120,128]{2,1,0:T(8,128)}, u32[]{:S(2)}) copy-start(f32[1,120,128]{2,1,0:T(8,128)} %get-tuple-element.115) | copy-start | bytes 184324
  39.6 2.7 %copy-start.9 = (f32[2,119,128]{2,1,0:T(8,128)S(1)}, f32[2,119,128]{2,1,0:T(8,128)}, u32[]{:S(2)}) copy-start(f32[2,119,128]{2,1,0:T(8,128)} %get-tuple-element.109) | copy-start | bytes 365572
  41.3 1.1 %copy-start.5 = (f32[2,118,128]{2,1,0:T(8,128)S(1)}, f32[2,118,128]{2,1,0:T(8,128)}, u32[]{:S(2)}) copy-start(f32[2,118,128]{2,1,0:T(8,128)} %get-tuple-element.107) | copy-start | bytes 362500
  41.3 1.1 %copy-start.6 = (f32[2,118,128]{2,1,0:T(8,128)S(1)}, f32[2,118,128]{2,1,0:T(8,128)}, u32[]{:S(2)}) copy-start(f32[2,118,128]{2,1,0:T(8,128)} %get-tuple-element.108) | copy-start | bytes 362500
  92.6 2.4 %copy-start.10 = (f32[2,120,128]{2,1,0:T(8,128)S(1)}, f32[2,120,128]{2,1,0:T(8,128)}, u32[]{:S(2)}) copy-start(f32[2,120,128]{2,1,0:T(8,128)} %get-tuple-element.21) | copy-start | bytes 368644
where the time goes:
time: 96.3 us; the launch traced here: 95.7 us
  blocking collectives  39.4 us (41%)
  other arithmetic  25.4 us (26%)
  local copies, waits for them, and re-layouts  15.2 us (16%)
  between operations  8.29 us (9%)
  starting transfers between devices  7.19 us (7%)
    psum x1, blocking collectives, local(): lax.psum((mass_before, mass_after, jnp.stack([local_prior_totals + edge_u...  39.4 us
    reduce_sum x1, other arithmetic, local(): mass_after = jnp.sum(tracer_new * regridded_depths, axis=(1, 2, 3))  7.73 us
    ppermute x4, starting transfers between devices, passed_along(): return lax.ppermute(value, axis, pairs)  7.19 us
    reduce_sum x1, other arithmetic, local(): jnp.sum(0.5 * (regridded_depths + jnp.concatenate([regridded_depths[:, :,...  3.62 us
    slice x14, local copies, waits for them, and re-layouts, shifted_layers(): return jnp.concatenate([filler, values[..., :layers + amount, :]], axis=-2)  2.64 us
    unnamed x33, local copies, waits for them, and re-layouts  2.56 us
    div x2, other arithmetic, multiply_by_regrid_operator(): (weight_first * mean_first + weight_second * mean_second) / (weight_first...  1.98 us
  transfers between devices with their start and end apart: 4, of which 1 were waited for; matrix products, arithmetic and copies ran while one was open for 28% of the time, Pallas kernels for 0%

commit v1 on v0

v1 whole, which is shorter than its diff:
```python
import functools

import jax
import jax.numpy as jnp
from jax import lax
from jax.experimental import pallas as pl
from jax.experimental.pallas import tpu as pltpu
from jax.sharding import PartitionSpec as P

MESH = pl.DeviceIdType.MESH
HEAT = 3.5
PAD = 8
F32 = jnp.float32
OFFSETS = (-2, -1, 0, 1, 2)


def choose(masks, options):
    keys = sorted(options)
    if len(keys) == len(OFFSETS):
        value = options[keys[-1]]
        keys = keys[:-1]
    else:
        value = jnp.zeros_like(options[keys[0]])
    for o in keys:
        value = jnp.where(masks[o], options[o], value)
    return value


def build_weights(depth_at, level, start, end, first_layer):
    layer = lax.broadcasted_iota(jnp.int32, level.shape, 0) + first_layer
    offset = level - layer
    masks = {o: offset == o for o in OFFSETS}
    depths = {o: depth_at(o) for o in range(-2, 4)}
    weight_first = (1.0 - start) * choose(masks, {o: depths[o] for o in OFFSETS})
    weight_second = end * choose(masks, {o: depths[o + 1] for o in OFFSETS})
    thick = weight_first + weight_second
    inverse = 1.0 / thick
    g1 = weight_first * inverse
    g2 = weight_second * inverse
    lin1 = 0.5 * (start + 1.0)
    sq1 = lin1 - (start * start + start + 1.0) * (1.0 / 3.0)
    lin2 = 0.5 * end
    sq2 = lin2 - end * end * (1.0 / 3.0)
    c_e0 = g1 * (1.0 - lin1 - 3.0 * sq1) * (1.0 / 12.0)
    c_e1 = (g1 * (lin1 - 3.0 * sq1) + g2 * (1.0 - lin2 - 3.0 * sq2)) * (1.0 / 12.0)
    c_e2 = g2 * (lin2 - 3.0 * sq2) * (1.0 / 12.0)
    taps = {
        -2: -c_e0,
        -1: 7.0 * c_e0 - c_e1,
        0: 7.0 * (c_e0 + c_e1) - c_e2 + 6.0 * (g1 * sq1),
        1: 7.0 * (c_e1 + c_e2) - c_e0 + 6.0 * (g2 * sq2),
        2: 7.0 * c_e2 - c_e1,
        3: -c_e2,
    }
    weights = {}
    for j in range(-4, 6):
        weights[j] = choose(masks, {o: taps[j - o] for o in OFFSETS if -2 <= j - o <= 3})
    return weights, thick


def remap(weights, load):
    terms = [weights[j] * load(j) for j in range(-4, 6)]
    while len(terms) > 1:
        terms = [
            terms[i] + terms[i + 1] if i + 1 < len(terms) else terms[i]
            for i in range(0, len(terms), 2)
        ]
    return terms[0]


def ghosts(near, second, third):
    return near + second - third, 12.0 * second - 4.0 * near - 7.0 * third


def pad_ends(buf, layers):
    row = lax.broadcasted_iota(jnp.int32, (PAD, buf.shape[-1]), 0)
    one, two = ghosts(
        buf[PAD : PAD + 1, :], buf[PAD + 1 : PAD + 2, :], buf[PAD + 2 : PAD + 3, :]
    )
    buf[0:PAD, :] = jnp.where(row == PAD - 1, one, jnp.where(row == PAD - 2, two, 0.0))
    last = PAD + layers
    one, two = ghosts(
        buf[last - 1 : last, :], buf[last - 2 : last - 1, :], buf[last - 3 : last - 2, :]
    )
    buf[last : last + PAD, :] = jnp.where(row == 0, one, jnp.where(row == 1, two, 0.0))


def main_kernel(
    nx,
    ny,
    q_hbm,
    u_hbm,
    v_hbm,
    w_hbm,
    d_hbm,
    l_hbm,
    a_hbm,
    b_hbm,
    tr_out,
    zonal_out,
    merid_out,
    warm_out,
    corr_out,
    q_raw,
    a_raw,
    b_raw,
    level,
    q_pad,
    u_pad,
    v_pad,
    vr_pad,
    vb_pad,
    w_pad,
    d_pad,
    a32,
    b32,
    thick_all,
    packed,
    n_depth,
    n_level,
    n_start,
    n_end,
    e_packed,
    sums,
    mine_x,
    mine_y,
    got_x,
    got_y,
    in_sem,
    send_sem,
    recv_sem,
    x_send,
    x_recv,
    y_send,
    y_recv,
):
    tracers, rows, layers, lanes = q_raw.shape
    gx = lax.axis_index("gx")
    gy = lax.axis_index("gy")
    body = pl.ds(PAD, layers)

    def x_peer(k):
        return {"gx": lax.rem(gx + k, nx)}

    def y_peer(k):
        return {"gy": lax.rem(gy + k, ny)}

    loads = [
        pltpu.make_async_copy(a_hbm, a_raw, in_sem.at[0]),
        pltpu.make_async_copy(b_hbm, b_raw, in_sem.at[1]),
        pltpu.make_async_copy(l_hbm, level, in_sem.at[2]),
        pltpu.make_async_copy(d_hbm, d_pad.at[:, body, :], in_sem.at[3]),
        pltpu.make_async_copy(v_hbm, v_pad.at[:, body, :], in_sem.at[4]),
        pltpu.make_async_copy(u_hbm, u_pad.at[:, body, :], in_sem.at[5]),
        pltpu.make_async_copy(w_hbm, w_pad.at[:, body, :], in_sem.at[6]),
        pltpu.make_async_copy(q_hbm, q_raw, in_sem.at[7]),
    ]
    for load in loads:
        load.start()

    barrier = pltpu.get_barrier_semaphore()
    for k in range(1, nx):
        pl.semaphore_signal(barrier, inc=1, device_id=x_peer(k), device_id_type=MESH)
    for k in range(1, ny):
        pl.semaphore_signal(barrier, inc=1, device_id=y_peer(k), device_id_type=MESH)

    for load in loads[:4]:
        load.wait()
    lane_full = lax.broadcasted_iota(jnp.int32, (layers, lanes), 1)
    for r in range(rows):
        a32[r] = a_raw[r].astype(F32)
        b32[r] = b_raw[r].astype(F32)
    column = jnp.zeros((layers, lanes), F32)
    for r in range(rows):
        parts = (d_pad[r, PAD : PAD + layers, :], level[r].astype(F32), a32[r], b32[r])
        for q, part in enumerate(parts):
            spot = q * rows + r
            moved = pltpu.roll(part, spot, 1) if spot else part
            column = jnp.where(lane_full == spot, moved, column)
    packed[...] = column

    pl.semaphore_wait(barrier, nx + ny - 2)
    pairs = [
        (packed, e_packed.at[body, :], x_peer(nx - 1)),
        (d_pad.at[0, body, :], n_depth.at[body, :], y_peer(ny - 1)),
        (level.at[0], n_level, y_peer(ny - 1)),
        (a32.at[0], n_start, y_peer(ny - 1)),
        (b32.at[0], n_end, y_peer(ny - 1)),
    ]
    sends = [
        pltpu.make_async_remote_copy(
            src_ref=src,
            dst_ref=dst,
            send_sem=send_sem.at[i],
            recv_sem=recv_sem.at[i],
            device_id=peer,
            device_id_type=MESH,
        )
        for i, (src, dst, peer) in enumerate(pairs)
    ]
    for send in sends:
        send.start()

    for load in loads[4:7]:
        load.wait()
    for r in range(rows):
        d_pad[r, 0:PAD, :] = jnp.zeros((PAD, lanes), F32)
        d_pad[r, PAD + layers : PAD + layers + PAD, :] = jnp.zeros((PAD, lanes), F32)
        pad_ends(v_pad.at[r], layers)
        pad_ends(u_pad.at[r], layers)
        pad_ends(w_pad.at[r], layers)
    lane_tall = lax.broadcasted_iota(jnp.int32, (layers + 2 * PAD, lanes), 1)
    last_faces = jnp.zeros((layers + 2 * PAD, lanes), F32)
    for r in range(rows):
        wind = v_pad[r]
        turned = pltpu.roll(wind, 1, 1)
        vr_pad[r] = turned
        moved = pltpu.roll(turned, r, 1) if r else turned
        last_faces = jnp.where(lane_tall == r, moved, last_faces)
    vb_pad[...] = last_faces
    loads[7].wait()
    for t in range(tracers):
        for r in range(rows):
            q_pad[t, r, PAD : PAD + layers, :] = q_raw[t, r].astype(F32)
            pad_ends(q_pad.at[t, r], layers)

    lane = lax.broadcasted_iota(jnp.int32, (8, lanes), 1)
    not_first = lane > 0
    not_last = lane < lanes - 1
    zero = jnp.zeros((8, lanes), F32)

    def tile_step(i, carry):
        masses, total, energy = carry
        masses = list(masses)
        k0 = pl.multiple_of(i * 8, 8)
        here = pl.ds(k0, 8)

        def at(ref, j):
            return ref[pl.ds(k0 + (PAD + j), 8), :]

        own_before = None
        thick_before = None
        for r in range(rows):
            weights, thick = build_weights(
                lambda o: at(d_pad.at[r], o), level[r, here, :], a32[r, here, :], b32[r, here, :], k0
            )
            depth = at(d_pad.at[r], 0)
            thick_all[r, here, :] = thick
            total = total + thick
            for t in range(tracers):
                new = remap(weights, lambda j: at(q_pad.at[t, r], j))
                tr_out[t, r, here, :] = new
                masses[t] = masses[t] + (depth * at(q_pad.at[t, r], 0) - thick * new)
            warm = remap(weights, lambda j: at(w_pad.at[r], j))
            warm_out[r, here, :] = warm
            energy = energy + HEAT * (depth * at(w_pad.at[r], 0) - thick * warm)
            u_here = at(u_pad.at[r], 0)
            squares = u_here * u_here
            own = remap(weights, lambda j: at(u_pad.at[r], j))
            after = zero
            if r > 0:
                u_back = at(u_pad.at[r - 1], 0)
                squares = squares + u_back * u_back
                cross = remap(weights, lambda j: at(u_pad.at[r - 1], j))
                zonal = 0.5 * (own_before + cross)
                zonal_out[r - 1, here, :] = zonal
                after = (thick_before + thick) * (zonal * zonal)
            own_before = own
            thick_before = thick
            v_here = at(v_pad.at[r], 0)
            v_west = at(vr_pad.at[r], 0)
            squares = squares + v_here * v_here + jnp.where(not_first, v_west * v_west, 0.0)
            own_v = remap(weights, lambda j: at(v_pad.at[r], j))
            cross_v = remap(weights, lambda j: at(vr_pad.at[r], j))
            east_v = jnp.where(not_last, pltpu.roll(cross_v, lanes - 1, 1), 0.0)
            east_thick = pltpu.roll(thick, lanes - 1, 1)
            merid = 0.5 * (own_v + east_v)
            merid_out[r, here, :] = merid
            after = after + jnp.where(not_last, (thick + east_thick) * (merid * merid), 0.0)
            energy = energy + 0.25 * (depth * squares - after)
        zonal_out[rows - 1, here, :] = own_before
        return tuple(masses), total, energy

    masses, total, energy = lax.fori_loop(
        0, layers // 8, tile_step, ((zero,) * tracers, zero, zero)
    )
    sums[...] = jnp.zeros(sums.shape, F32)
    for t in range(tracers):
        sums[t : t + 1, :] = jnp.sum(masses[t], axis=0, keepdims=True)
    sums[tracers : tracers + 1, :] = jnp.sum(total, axis=0, keepdims=True)

    for send in sends:
        send.wait_recv()

    def edge_step(i, energy):
        k0 = pl.multiple_of(i * 8, 8)
        here = pl.ds(k0, 8)

        def at(ref, j):
            return ref[pl.ds(k0 + (PAD + j), 8), :]

        weights, thick = build_weights(
            lambda o: at(n_depth, o), n_level[here, :], n_start[here, :], n_end[here, :], k0
        )
        u_last = at(u_pad.at[rows - 1], 0)
        cross = remap(weights, lambda j: at(u_pad.at[rows - 1], j))
        zonal = 0.5 * (zonal_out[rows - 1, here, :] + cross)
        zonal_out[rows - 1, here, :] = zonal
        change = at(n_depth, 0) * (u_last * u_last) - (
            thick_all[rows - 1, here, :] + thick
        ) * (zonal * zonal)

        column = at(e_packed, 0)
        weights, thick = build_weights(
            lambda o: at(e_packed, o),
            pltpu.roll(column, lanes - rows, 1).astype(jnp.int32),
            pltpu.roll(column, lanes - 2 * rows, 1),
            pltpu.roll(column, lanes - 3 * rows, 1),
            k0,
        )
        cross = remap(weights, lambda j: at(vb_pad, j))
        face = at(vb_pad, 0)
        change = change + jnp.where(lane < rows, column * (face * face), 0.0)
        for r in range(rows):
            there = pltpu.roll(cross, lanes - 1 - r, 1)
            there_thick = pltpu.roll(thick, lanes - 1 - r, 1)
            merid = merid_out[r, here, :] + jnp.where(not_last, 0.0, 0.5 * there)
            merid_out[r, here, :] = merid
            change = change - jnp.where(
                not_last, 0.0, (thick_all[r, here, :] + there_thick) * (merid * merid)
            )
        return energy + 0.25 * change

    energy = lax.fori_loop(0, layers // 8, edge_step, energy)
    sums[tracers + 1 : tracers + 2, :] = jnp.sum(energy, axis=0, keepdims=True)

    wide = sums.shape
    diagonal = lax.broadcasted_iota(jnp.int32, wide, 0) == lax.broadcasted_iota(jnp.int32, wide, 1)
    column = jnp.sum(sums[...], axis=1, keepdims=True)
    mine_x[...] = jnp.sum(jnp.where(diagonal, column, 0.0), axis=0, keepdims=True)

    def gather(count, peer, mine, got, s_sem, r_sem):
        copies = [
            pltpu.make_async_remote_copy(
                src_ref=mine,
                dst_ref=got.at[k - 1],
                send_sem=s_sem.at[k - 1],
                recv_sem=r_sem.at[k - 1],
                device_id=peer(k),
                device_id_type=MESH,
            )
            for k in range(1, count)
        ]
        for copy in copies:
            copy.start()
        for copy in copies:
            copy.wait_recv()
        value = mine[...]
        for k in range(count - 1):
            value = value + got[k]
        return value, copies

    value, first_copies = gather(nx, x_peer, mine_x, got_x, x_send, x_recv)
    mine_y[...] = value
    value, second_copies = gather(ny, y_peer, mine_y, got_y, y_send, y_recv)

    spread = jnp.sum(jnp.where(diagonal, value, 0.0), axis=1, keepdims=True)
    total_new = spread[tracers : tracers + 1, :]
    change = spread / total_new
    index = lax.broadcasted_iota(jnp.int32, change.shape, 0)
    change = jnp.where(index == tracers + 1, change * (1.0 / HEAT), change)
    corr_out[...] = jnp.broadcast_to(change, corr_out.shape)
    for send in sends:
        send.wait_send()
    for copy in first_copies + second_copies:
        copy.wait_send()


def finish_kernel(
    tr,
    zonal,
    merid,
    warm,
    corr,
    tr_hbm,
    zonal_hbm,
    merid_hbm,
    warm_hbm,
    tr_buf,
    warm_buf,
    sem,
):
    tracers = tr.shape[0]
    copies = [
        pltpu.make_async_copy(zonal, zonal_hbm, sem.at[tracers]),
        pltpu.make_async_copy(merid, merid_hbm, sem.at[tracers + 1]),
    ]
    for copy in copies:
        copy.start()
    for t in range(tracers):
        tr_buf[t] = tr[t] + corr[t : t + 1, :][None]
        copy = pltpu.make_async_copy(tr_buf.at[t], tr_hbm.at[t], sem.at[t])
        copy.start()
        copies.append(copy)
    warm_buf[...] = warm[...] + corr[tracers + 1 : tracers + 2, :][None]
    copy = pltpu.make_async_copy(warm_buf, warm_hbm, sem.at[tracers + 2])
    copy.start()
    copies.append(copy)
    for copy in copies:
        copy.wait()


def local(nx, ny, q, u, v, w, d, level, a, b):
    tracers, rows, layers, lanes = q.shape
    tall = layers + 2 * PAD
    plane = (rows, layers, lanes)
    sum_rows = -(-(tracers + 2) // 8) * 8
    vmem = pltpu.VMEM
    dma = pltpu.SemaphoreType.DMA
    anywhere = pl.BlockSpec(memory_space=pl.ANY)
    inside = pl.BlockSpec(memory_space=vmem)
    middle = pl.pallas_call(
        functools.partial(main_kernel, nx, ny),
        name="remap_main",
        out_shape=[
            vmem((tracers,) + plane, F32),
            vmem(plane, F32),
            vmem(plane, F32),
            vmem(plane, F32),
            vmem((sum_rows, lanes), F32),
        ],
        in_specs=[anywhere] * 8,
        out_specs=[inside] * 5,
        scratch_shapes=[
            vmem((tracers,) + plane, jnp.bfloat16),
            vmem(plane, jnp.bfloat16),
            vmem(plane, jnp.bfloat16),
            vmem(plane, jnp.int32),
            vmem((tracers, rows, tall, lanes), F32),
            vmem((rows, tall, lanes), F32),
            vmem((rows, tall, lanes), F32),
            vmem((rows, tall, lanes), F32),
            vmem((tall, lanes), F32),
            vmem((rows, tall, lanes), F32),
            vmem((rows, tall, lanes), F32),
            vmem(plane, F32),
            vmem(plane, F32),
            vmem(plane, F32),
            vmem((layers, lanes), F32),
            vmem((tall, lanes), F32),
            vmem((layers, lanes), jnp.int32),
            vmem((layers, lanes), F32),
            vmem((layers, lanes), F32),
            vmem((tall, lanes), F32),
            vmem((sum_rows, lanes), F32),
            vmem((1, lanes), F32),
            vmem((1, lanes), F32),
            vmem((nx - 1, 1, lanes), F32),
            vmem((ny - 1, 1, lanes), F32),
            dma((8,)),
            dma((5,)),
            dma((5,)),
            dma((nx - 1,)),
            dma((nx - 1,)),
            dma((ny - 1,)),
            dma((ny - 1,)),
        ],
        compiler_params=pltpu.CompilerParams(collective_id=0, has_side_effects=True),
    )(q, u, v, w, d, level, a, b)
    return tuple(
        pl.pallas_call(
            finish_kernel,
            name="remap_finish",
            out_shape=[
                jax.ShapeDtypeStruct((tracers,) + plane, F32),
                jax.ShapeDtypeStruct(plane, F32),
                jax.ShapeDtypeStruct(plane, F32),
                jax.ShapeDtypeStruct(plane, F32),
            ],
            in_specs=[inside] * 5,
            out_specs=[anywhere] * 4,
            scratch_shapes=[
                vmem((tracers,) + plane, F32),
                vmem(plane, F32),
                dma((tracers + 3,)),
            ],
        )(*middle)
    )


def solution(mesh):
    flat = P("gy", None, "gx")
    tall = P(None, "gy", None, "gx")
    return jax.shard_map(
        functools.partial(local, mesh.shape["gx"], mesh.shape["gy"]),
        mesh=mesh,
        in_specs=(tall,) + (flat,) * 7,
        out_specs=(tall,) + (flat,) * 3,
        check_vma=False,
    )
```

time: 96.3 us -> 27 us (0.28)
  blocking collectives: 39.4 us -> 0 us
  other arithmetic: 25.4 us -> 0 us
  Pallas kernels: 0 us -> 22.7 us
  local copies, waits for them, and re-layouts: 15.2 us -> 3.5 us
  between operations: 8.29 us -> 0.65 us
  starting transfers between devices: 7.19 us -> 0 us
    psum x1 -> x0, blocking collectives: 39.4 us -> none  [local(): lax.psum((mass_before, mass_after, jnp.stack([local_prior_totals + edge_u...]
    pallas_call x0 -> x2, Pallas kernels: none -> 22.7 us  [the longest x1 20.2 us: local(): pl.pallas_call(functools.partial(main_kernel, nx, ny), name='remap_main',...]
    reduce_sum x5 -> x0, other arithmetic: 14.4 us -> none  [the longest x1 7.73 us: local(): mass_after = jnp.sum(tracer_new * regridded_depths, axis=(1, 2, 3))]
    slice x32 -> x0, local copies, waits for them, and re-layouts: 10.1 us -> none  [the longest x14 2.64 us: shifted_layers(): return jnp.concatenate([filler, values[..., :layers + amount, :]], axis=-2)]
    ppermute x4 -> x0, starting transfers between devices: 7.19 us -> none  [passed_along(): return lax.ppermute(value, axis, pairs)]
    div x3 -> x0, other arithmetic: 2.63 us -> none  [the longest x2 1.98 us: multiply_by_regrid_operator(): (weight_first * mean_first + weight_second * mean_second) / (weight_first...]
    squeeze x6 -> x0, local copies, waits for them, and re-layouts: 2.58 us -> none  [the longest x1 0.87 us: local(): returned[0]]
    another operation x5 -> x0, other arithmetic: 2.25 us -> none  [the longest x1 0.84 us: local(): jnp.stack([zonal_edge_velocity, jnp.concatenate([from_south, zonal_edge_v...]
  transfers between devices with their start and end apart: 4 -> 0, of which waited for: 1 -> 0; matrix products, arithmetic and copies ran while one was open for 28% -> 0% of each run, Pallas kernels for 0% -> 0%
where the time goes in v1:
time: 27 us; the launch traced here: 26.8 us
  Pallas kernels  22.7 us (84%)
  local copies, waits for them, and re-layouts  3.5 us (13%)
  between operations  0.65 us (2%)
    pallas_call x1, Pallas kernels, local(): pl.pallas_call(functools.partial(main_kernel, nx, ny), name='remap_main',...  20.2 us
    unnamed x10, local copies, waits for them, and re-layouts  3.5 us
    pallas_call x1, Pallas kernels, local(): pl.pallas_call(finish_kernel, name='remap_finish', out_shape=[jax.ShapeDt...  2.48 us

profile of v1, /device:TPU:0, one launch (start us, length us, event | category | flops | bytes accessed | tf_op | source)
XLA Modules:
  0.0 26.8 jit_solution(9791164126963138594)
XLA Ops:
  0.6 20.2 %remap_main.1 = (f32[8,2,120,128]{3,2,1,0:T(8,128)S(1)}, f32[2,120,128]{2,1,0:T(8,128)S(1)}, f32[2,120,128]{2,1,0:T(8,128)S(1)}, f32[2,120,128]{2,1,0:T(8,128)S(1)}, f32[16,128]{1,0:T(8,128)S(1)}) custom-call(bf16[8,2,120,128]{3,2,1,0:T(8,128)(2,1)} %q_hbm.1, f32[2,120,128]{2,1,0:T(8,128)} %u_hbm.1, f32[2,120,128]{2,1,0:T(8,128)} %v_hbm.1, ...), custom_call_target="tpu_custom_call" | custom-call | tf_op jit(solution)/shard_map/remap_main/pallas_call | solution.py:422
  20.8 0.0 copy-start
  20.8 0.9 %copy-done = f32[8,2,120,128]{3,2,1,0:T(8,128)} copy-done((f32[8,2,120,128]{3,2,1,0:T(8,128)}, f32[8,2,120,128]{3,2,1,0:T(8,128)S(1)}, u32[]{:S(2)}) %copy-start) | copy-done | bytes 983064
  21.8 0.0 copy-start.1
  21.8 0.6 %copy-done.1 = f32[2,120,128]{2,1,0:T(8,128)} copy-done((f32[2,120,128]{2,1,0:T(8,128)}, f32[2,120,128]{2,1,0:T(8,128)S(1)}, u32[]{:S(2)}) %copy-start.1) | copy-done | bytes 122904
  22.4 0.0 copy-start.2
  22.4 0.7 %copy-done.2 = f32[2,120,128]{2,1,0:T(8,128)} copy-done((f32[2,120,128]{2,1,0:T(8,128)}, f32[2,120,128]{2,1,0:T(8,128)S(1)}, u32[]{:S(2)}) %copy-start.2) | copy-done | bytes 122904
  23.1 0.0 copy-start.3
  23.1 0.6 %copy-done.3 = f32[2,120,128]{2,1,0:T(8,128)} copy-done((f32[2,120,128]{2,1,0:T(8,128)}, f32[2,120,128]{2,1,0:T(8,128)S(1)}, u32[]{:S(2)}) %copy-start.3) | copy-done | bytes 122904
  23.7 0.0 copy-start.4
  23.7 0.6 %copy-done.4 = f32[16,128]{1,0:T(8,128)} copy-done((f32[16,128]{1,0:T(8,128)}, f32[16,128]{1,0:T(8,128)S(1)}, u32[]{:S(2)}) %copy-start.4) | copy-done | bytes 8216
  24.3 2.5 %remap_finish.1 = (f32[8,2,120,128]{3,2,1,0:T(8,128)}, f32[2,120,128]{2,1,0:T(8,128)}, f32[2,120,128]{2,1,0:T(8,128)}, f32[2,120,128]{2,1,0:T(8,128)}) custom-call(f32[8,2,120,128]{3,2,1,0:T(8,128)} %copy-done, f32[2,120,128]{2,1,0:T(8,128)} %copy-done.1, f32[2,120,128]{2,1,0:T(8,128)} %copy-done.2, f32[2,120,128]{2,1,0:T(8,128)} %copy-done.3, ...), custom_call_target="tpu_custom_call" | custom-call | tf_op jit(solution)/shard_map/remap_finish/pallas_call | solution.py:471
Async XLA Ops:
  20.8 1.0 %copy-start = (f32[8,2,120,128]{3,2,1,0:T(8,128)}, f32[8,2,120,128]{3,2,1,0:T(8,128)S(1)}, u32[]{:S(2)}) copy-start(f32[8,2,120,128]{3,2,1,0:T(8,128)S(1)} %get-tuple-element.9.tr) | copy-start | bytes 2949124
  21.8 0.6 %copy-start.1 = (f32[2,120,128]{2,1,0:T(8,128)}, f32[2,120,128]{2,1,0:T(8,128)S(1)}, u32[]{:S(2)}) copy-start(f32[2,120,128]{2,1,0:T(8,128)S(1)} %get-tuple-element.10.zonal) | copy-start | bytes 368644
  22.4 0.7 %copy-start.2 = (f32[2,120,128]{2,1,0:T(8,128)}, f32[2,120,128]{2,1,0:T(8,128)S(1)}, u32[]{:S(2)}) copy-start(f32[2,120,128]{2,1,0:T(8,128)S(1)} %get-tuple-element.11.merid) | copy-start | bytes 368644
  23.1 0.7 %copy-start.3 = (f32[2,120,128]{2,1,0:T(8,128)}, f32[2,120,128]{2,1,0:T(8,128)S(1)}, u32[]{:S(2)}) copy-start(f32[2,120,128]{2,1,0:T(8,128)S(1)} %get-tuple-element.12.warm) | copy-start | bytes 368644
  23.7 0.6 %copy-start.4 = (f32[16,128]{1,0:T(8,128)}, f32[16,128]{1,0:T(8,128)S(1)}, u32[]{:S(2)}) copy-start(f32[16,128]{1,0:T(8,128)S(1)} %get-tuple-element.13.corr) | copy-start | bytes 24580

commit v2 on v1

--- a/solution.py
+++ b/solution.py
@@ -484,7 +484,7 @@
                 vmem(plane, F32),
                 dma((tracers + 3,)),
             ],
-        )(*middle)
+        )(*[pltpu.with_memory_space_constraint(x, vmem) for x in middle])
     )
 
 

time: 27 us -> 22.1 us (0.82)
  local copies, waits for them, and re-layouts: 3.5 us -> 0 us
  Pallas kernels: 22.7 us -> 21.3 us
    unnamed x10 -> x0, local copies, waits for them, and re-layouts: 3.5 us -> none
    pallas_call x1, Pallas kernels: 2.48 us -> 1.15 us  [local(): pl.pallas_call(finish_kernel, name='remap_finish', out_shape=[jax.ShapeDt...]
where the time goes in v2:
time: 22.1 us; the launch traced here: 22 us
  Pallas kernels  21.3 us (96%)
  between operations  0.64 us (3%)
    pallas_call x1, Pallas kernels, local(): pl.pallas_call(functools.partial(main_kernel, nx, ny), name='remap_main',...  20.2 us
    pallas_call x1, Pallas kernels, local(): pl.pallas_call(finish_kernel, name='remap_finish', out_shape=[jax.ShapeDt...  1.15 us

profile of v2, /device:TPU:0, one launch (start us, length us, event | category | flops | bytes accessed | tf_op | source)
XLA Modules:
  0.0 22.0 jit_solution(16833487021787006132)
XLA Ops:
  0.6 20.2 %remap_main.1 = (f32[8,2,120,128]{3,2,1,0:T(8,128)S(1)}, f32[2,120,128]{2,1,0:T(8,128)S(1)}, f32[2,120,128]{2,1,0:T(8,128)S(1)}, f32[2,120,128]{2,1,0:T(8,128)S(1)}, f32[16,128]{1,0:T(8,128)S(1)}) custom-call(bf16[8,2,120,128]{3,2,1,0:T(8,128)(2,1)} %q_hbm.1, f32[2,120,128]{2,1,0:T(8,128)} %u_hbm.1, f32[2,120,128]{2,1,0:T(8,128)} %v_hbm.1, ...), custom_call_target="tpu_custom_call" | custom-call | tf_op jit(solution)/shard_map/remap_main/pallas_call | solution.py:422
  20.8 1.1 %remap_finish.1 = (f32[8,2,120,128]{3,2,1,0:T(8,128)}, f32[2,120,128]{2,1,0:T(8,128)}, f32[2,120,128]{2,1,0:T(8,128)}, f32[2,120,128]{2,1,0:T(8,128)}) custom-call(f32[8,2,120,128]{3,2,1,0:T(8,128)S(1)} %get-tuple-element.9.tr, f32[2,120,128]{2,1,0:T(8,128)S(1)} %get-tuple-element.10.zonal, f32[2,120,128]{2,1,0:T(8,128)S(1)} %get-tuple-element.11.merid, ...), custom_call_target="tpu_custom_call" | custom-call | tf_op jit(solution)/shard_map/remap_finish/pallas_call | solution.py:471

commit v3 on v2

--- a/solution.py
+++ b/solution.py
@@ -10,6 +10,9 @@
 MESH = pl.DeviceIdType.MESH
 HEAT = 3.5
 PAD = 8
+DIRECT = 64
+EARLY = 0
+HELLOS = 4
 F32 = jnp.float32
 OFFSETS = (-2, -1, 0, 1, 2)
 
@@ -83,6 +86,33 @@
         buf[last - 1 : last, :], buf[last - 2 : last - 1, :], buf[last - 3 : last - 2, :]
     )
     buf[last : last + PAD, :] = jnp.where(row == 0, one, jnp.where(row == 1, two, 0.0))
+
+
+def one_step(nx, ny):
+    return nx * ny <= DIRECT
+
+
+def greeting_rounds(nx, ny):
+    def around(steps):
+        return sorted({(x % nx, y % ny) for x, y in steps} - {(0, 0)})
+
+    first = around([(1, 0), (-1, 0), (0, 1), (0, -1)])
+    known = {(0, 0)} | set(first)
+    rounds = []
+    while len(known) < nx * ny:
+        told = first
+        if rounds:
+            told = [p for p in around([(2, 0), (-2, 0), (0, 2), (0, -2)]) if p in known]
+        more = {((p[0] + x) % nx, (p[1] + y) % ny) for p in told for x, y in known} | known
+        slim_told = [p for p in told if p[0] == 0]
+        slim = {((p[0] + x) % nx, (p[1] + y) % ny) for p in slim_told for x, y in known} | known
+        if len(slim) == nx * ny:
+            told, more = slim_told, slim
+        if len(more) == len(known):
+            return None, None
+        rounds.append(told)
+        known = more
+    return first, rounds
 
 
 def main_kernel(
@@ -129,10 +159,9 @@
     in_sem,
     send_sem,
     recv_sem,
-    x_send,
-    x_recv,
-    y_send,
-    y_recv,
+    x_sem,
+    y_sem,
+    hello,
 ):
     tracers, rows, layers, lanes = q_raw.shape
     gx = lax.axis_index("gx")
@@ -144,6 +173,33 @@
 
     def y_peer(k):
         return {"gy": lax.rem(gy + k, ny)}
+
+    def at_steps(p):
+        place = {}
+        if p[0]:
+            place.update(x_peer(p[0]))
+        if p[1]:
+            place.update(y_peer(p[1]))
+        return place
+
+    def greet(n):
+        if n < len(rounds):
+            for p in rounds[n]:
+                pl.semaphore_signal(
+                    hello.at[n], inc=1, device_id=at_steps(p), device_id_type=MESH
+                )
+
+    def hear(n):
+        if 0 <= n < len(rounds):
+            pl.semaphore_wait(hello.at[n], len(rounds[n]))
+
+    def peer_groups():
+        along_x = [x_peer(k) for k in range(1, nx)]
+        along_y = [y_peer(k) for k in range(1, ny)]
+        if not one_step(nx, ny):
+            return [along_x, along_y]
+        both = [{**x, **y} for x in along_x for y in along_y]
+        return [both + along_y + along_x]
 
     loads = [
         pltpu.make_async_copy(a_hbm, a_raw, in_sem.at[0]),
@@ -159,10 +215,14 @@
         load.start()
 
     barrier = pltpu.get_barrier_semaphore()
-    for k in range(1, nx):
-        pl.semaphore_signal(barrier, inc=1, device_id=x_peer(k), device_id_type=MESH)
-    for k in range(1, ny):
-        pl.semaphore_signal(barrier, inc=1, device_id=y_peer(k), device_id_type=MESH)
+    first_met, rounds = greeting_rounds(nx, ny) if one_step(nx, ny) else (None, None)
+    if rounds is None:
+        greeted = [peer for group in peer_groups() for peer in group]
+        rounds = []
+    else:
+        greeted = [at_steps(p) for p in first_met]
+    for peer in greeted:
+        pl.semaphore_signal(barrier, inc=1, device_id=peer, device_id_type=MESH)
 
     for load in loads[:4]:
         load.wait()
@@ -178,28 +238,6 @@
             moved = pltpu.roll(part, spot, 1) if spot else part
             column = jnp.where(lane_full == spot, moved, column)
     packed[...] = column
-
-    pl.semaphore_wait(barrier, nx + ny - 2)
-    pairs = [
-        (packed, e_packed.at[body, :], x_peer(nx - 1)),
-        (d_pad.at[0, body, :], n_depth.at[body, :], y_peer(ny - 1)),
-        (level.at[0], n_level, y_peer(ny - 1)),
-        (a32.at[0], n_start, y_peer(ny - 1)),
-        (b32.at[0], n_end, y_peer(ny - 1)),
-    ]
-    sends = [
-        pltpu.make_async_remote_copy(
-            src_ref=src,
-            dst_ref=dst,
-            send_sem=send_sem.at[i],
-            recv_sem=recv_sem.at[i],
-            device_id=peer,
-            device_id_type=MESH,
-        )
-        for i, (src, dst, peer) in enumerate(pairs)
-    ]
-    for send in sends:
-        send.start()
 
     for load in loads[4:7]:
         load.wait()
@@ -281,9 +319,40 @@
         zonal_out[rows - 1, here, :] = own_before
         return tuple(masses), total, energy
 
-    masses, total, energy = lax.fori_loop(
-        0, layers // 8, tile_step, ((zero,) * tracers, zero, zero)
-    )
+    tiles = layers // 8
+    early = min(EARLY, tiles)
+    carry = lax.fori_loop(0, early, tile_step, ((zero,) * tracers, zero, zero))
+    pl.semaphore_wait(barrier, len(greeted))
+    pairs = [
+        (packed, e_packed.at[body, :], x_peer(nx - 1)),
+        (d_pad.at[0, body, :], n_depth.at[body, :], y_peer(ny - 1)),
+        (level.at[0], n_level, y_peer(ny - 1)),
+        (a32.at[0], n_start, y_peer(ny - 1)),
+        (b32.at[0], n_end, y_peer(ny - 1)),
+    ]
+    sends = [
+        pltpu.make_async_remote_copy(
+            src_ref=src,
+            dst_ref=dst,
+            send_sem=send_sem.at[i],
+            recv_sem=recv_sem.at[i],
+            device_id=peer,
+            device_id_type=MESH,
+        )
+        for i, (src, dst, peer) in enumerate(pairs)
+    ]
+    for send in sends:
+        send.start()
+
+    greet(0)
+    pieces = max(len(rounds), 1)
+    marks = [early + (tiles - early) * n // pieces for n in range(pieces + 1)]
+    for n in range(pieces):
+        carry = lax.fori_loop(marks[n], marks[n + 1], tile_step, carry)
+        if n + 1 < pieces:
+            hear(n)
+            greet(n + 1)
+    masses, total, energy = carry
     sums[...] = jnp.zeros(sums.shape, F32)
     for t in range(tracers):
         sums[t : t + 1, :] = jnp.sum(masses[t], axis=0, keepdims=True)
@@ -339,30 +408,40 @@
     column = jnp.sum(sums[...], axis=1, keepdims=True)
     mine_x[...] = jnp.sum(jnp.where(diagonal, column, 0.0), axis=0, keepdims=True)
 
-    def gather(count, peer, mine, got, s_sem, r_sem):
+    def gather(peers, mine, got, sems):
         copies = [
             pltpu.make_async_remote_copy(
                 src_ref=mine,
-                dst_ref=got.at[k - 1],
-                send_sem=s_sem.at[k - 1],
-                recv_sem=r_sem.at[k - 1],
-                device_id=peer(k),
+                dst_ref=got.at[k],
+                send_sem=sems.at[0],
+                recv_sem=sems.at[1],
+                device_id=peer,
                 device_id_type=MESH,
             )
-            for k in range(1, count)
+            for k, peer in enumerate(peers)
         ]
         for copy in copies:
             copy.start()
-        for copy in copies:
-            copy.wait_recv()
-        value = mine[...]
-        for k in range(count - 1):
-            value = value + got[k]
-        return value, copies
-
-    value, first_copies = gather(nx, x_peer, mine_x, got_x, x_send, x_recv)
-    mine_y[...] = value
-    value, second_copies = gather(ny, y_peer, mine_y, got_y, y_send, y_recv)
+        everything = pltpu.make_async_remote_copy(
+            src_ref=got,
+            dst_ref=got,
+            send_sem=sems.at[0],
+            recv_sem=sems.at[1],
+            device_id=peers[0],
+            device_id_type=MESH,
+        )
+        everything.wait_recv()
+        value = mine[...] + jnp.sum(got[...], axis=0)
+        return value, everything
+
+    hear(len(rounds) - 1)
+    groups = peer_groups()
+    value, first = gather(groups[0], mine_x, got_x, x_sem)
+    ends = [first]
+    if len(groups) > 1:
+        mine_y[...] = value
+        value, second = gather(groups[1], mine_y, got_y, y_sem)
+        ends.append(second)
 
     spread = jnp.sum(jnp.where(diagonal, value, 0.0), axis=1, keepdims=True)
     total_new = spread[tracers : tracers + 1, :]
@@ -372,8 +451,8 @@
     corr_out[...] = jnp.broadcast_to(change, corr_out.shape)
     for send in sends:
         send.wait_send()
-    for copy in first_copies + second_copies:
-        copy.wait_send()
+    for end in ends:
+        end.wait_send()
 
 
 def finish_kernel(
@@ -455,15 +534,14 @@
             vmem((sum_rows, lanes), F32),
             vmem((1, lanes), F32),
             vmem((1, lanes), F32),
-            vmem((nx - 1, 1, lanes), F32),
+            vmem((nx * ny - 1 if one_step(nx, ny) else nx - 1, 1, lanes), F32),
             vmem((ny - 1, 1, lanes), F32),
             dma((8,)),
             dma((5,)),
             dma((5,)),
-            dma((nx - 1,)),
-            dma((nx - 1,)),
-            dma((ny - 1,)),
-            dma((ny - 1,)),
+            dma((2,)),
+            dma((2,)),
+            pltpu.SemaphoreType.REGULAR((HELLOS,)),
         ],
         compiler_params=pltpu.CompilerParams(collective_id=0, has_side_effects=True),
     )(q, u, v, w, d, level, a, b)

time: 22.1 us -> 20.2 us (0.914)
  Pallas kernels: 21.3 us -> 19.4 us
    pallas_call x1, Pallas kernels: 20.2 us -> 18.2 us  [local(): pl.pallas_call(functools.partial(main_kernel, nx, ny), name='remap_main',...]
where the time goes in v3:
time: 20.2 us; the launch traced here: 20 us
  Pallas kernels  19.4 us (96%)
  between operations  0.64 us (3%)
    pallas_call x1, Pallas kernels, local(): pl.pallas_call(functools.partial(main_kernel, nx, ny), name='remap_main',...  18.2 us
    pallas_call x1, Pallas kernels, local(): pl.pallas_call(finish_kernel, name='remap_finish', out_shape=[jax.ShapeDt...  1.15 us

profile of v3, /device:TPU:0, one launch (start us, length us, event | category | flops | bytes accessed | tf_op | source)
XLA Modules:
  0.0 20.0 jit_solution(10452798330317704478)
XLA Ops:
  0.6 18.2 %remap_main.1 = (f32[8,2,120,128]{3,2,1,0:T(8,128)S(1)}, f32[2,120,128]{2,1,0:T(8,128)S(1)}, f32[2,120,128]{2,1,0:T(8,128)S(1)}, f32[2,120,128]{2,1,0:T(8,128)S(1)}, f32[16,128]{1,0:T(8,128)S(1)}) custom-call(bf16[8,2,120,128]{3,2,1,0:T(8,128)(2,1)} %q_hbm.1, f32[2,120,128]{2,1,0:T(8,128)} %u_hbm.1, f32[2,120,128]{2,1,0:T(8,128)} %v_hbm.1, ...), custom_call_target="tpu_custom_call" | custom-call | tf_op jit(solution)/shard_map/remap_main/pallas_call | solution.py:501
  18.9 1.1 %remap_finish.1 = (f32[8,2,120,128]{3,2,1,0:T(8,128)}, f32[2,120,128]{2,1,0:T(8,128)}, f32[2,120,128]{2,1,0:T(8,128)}, f32[2,120,128]{2,1,0:T(8,128)}) custom-call(f32[8,2,120,128]{3,2,1,0:T(8,128)S(1)} %get-tuple-element.9.tr, f32[2,120,128]{2,1,0:T(8,128)S(1)} %get-tuple-element.10.zonal, f32[2,120,128]{2,1,0:T(8,128)S(1)} %get-tuple-element.11.merid, ...), custom_call_target="tpu_custom_call" | custom-call | tf_op jit(solution)/shard_map/remap_finish/pallas_call | solution.py:549
